TPU v7x, 32 devices: a 4x4x1 block of a 4x4x8 slice. The times are simulated.
32 devices in a mesh: dp: 1 (over z), ri: 4 (over y), co: 4 (over x), ro: 2 (over core).
Axes of the slice: x: 4, y: 4, z: 1, core: 2. Of those that a mesh axis runs over, the one named last changes fastest.
The devices are a block of a 4x4x8 slice.
Arguments:
- a_mat: bfloat16 [3072, 16384], P(('dp', 'ri', 'ro'), 'co')
- b_mat: bfloat16 [16384, 24576], P(('dp', 'ri', 'ro'), 'co')
Outputs:
- output: bfloat16 [3072, 24576], P(('dp', 'ri', 'ro'), 'co')
All inputs are finite; a program needn't handle non-finite values.
Results may differ from a plain program's by a relative error of at most 0.001.
Values are sent between devices in bfloat16 or wider.
A program may use at most 768 MiB of HBM per device.

v0:
```python
import jax
import jax.numpy as jnp
from jax import lax
from jax.sharding import PartitionSpec as P, NamedSharding


def solution(mesh):
    grid_spec = P(("dp", "ri", "ro"), "co")

    def local_block(a_block, b_block):
        a_rows = lax.all_gather(a_block, "co", axis=1, tiled=True)
        b_cols = lax.all_gather(b_block, ("ri", "ro"), axis=0, tiled=True)
        product = jnp.dot(a_rows, b_cols, preferred_element_type=jnp.float32)
        return product.astype(jnp.bfloat16)

    return jax.shard_map(local_block, mesh=mesh, in_specs=(grid_spec, grid_spec), out_specs=grid_spec, check_vma=False)
```

profile of v0, /device:TPU:97, one launch (start us, length us, event | category | flops | bytes accessed | tf_op | source)
XLA Modules:
  0.0 1087.8 jit_solution(9069166396829405189)
XLA Ops:
  6.5 0.0 all-gather.3.cloned.1.call-start
  6.6 0.7 all-gather.3.cloned.1.call-update
  7.3 0.1 all-gather.5.cloned.1.call-start
  7.4 0.7 all-gather.5.cloned.1.call-update
  8.1 121.0 %all-gather.3.cloned.1.call-done = bf16[384,16384]{1,0:T(8,128)(2,1)} async-done(((bf16[384,4096]{1,0:T(8,128)(2,1)}), bf16[384,16384]{1,0:T(8,128)(2,1)}) %all-gather.3.cloned.1.call-update) | async-done | bytes 12582928 | tf_op jit(solution)/shard_map/all_gather | solution.py:11
  129.2 861.5 %all-gather.5.cloned.1.call-done = bf16[16384,6144]{1,0:T(8,128)(2,1)} async-done(((bf16[2048,6144]{1,0:T(8,128)(2,1)}), bf16[16384,6144]{1,0:T(8,128)(2,1)}) %all-gather.5.cloned.1.call-update) | async-done | bytes 201326608 | tf_op jit(solution)/shard_map/all_gather | solution.py:12
  990.6 90.3 %convolution_convert_fusion = bf16[384,6144]{1,0:T(8,128)(2,1)} fusion(bf16[384,16384]{1,0:T(8,128)(2,1)} %all-gather.3.cloned.1.call-done, bf16[16384,6144]{1,0:T(8,128)(2,1)} %all-gather.5.cloned.1.call-done), kind=kOutput, calls=%fused_computation | convolution fusion | flops 77311770624 | bytes 218628096 | tf_op jit(solution)/shard_map/dot_general | solution.py:13
Async XLA Ops:
  6.5 122.6 %all-gather.3.cloned.1.call-start = ((), (), s32[]{:S(2)}) async-start(), calls=%async_computation | async-start | bytes 15728640 | tf_op jit(solution)/shard_map/all_gather | solution.py:11
  7.3 983.3 %all-gather.5.cloned.1.call-start = ((), (), s32[]{:S(2)}) async-start(), calls=%async_computation.1 | async-start | bytes 226492416 | tf_op jit(solution)/shard_map/all_gather | solution.py:12
Sparse Core Ops, SparseCore 0:
  8.9 120.1 all-gather.2
  130.8 859.8 all-gather.4
where the time goes:
time: 1090 us
  waiting for transfers between devices  984 us (90%)
  matrix products  90.3 us (8%)
  between operations  13.4 us (1%)
    all_gather x1, waiting for transfers between devices, local_block(): b_cols = lax.all_gather(b_block, ('ri', 'ro'), axis=0, tiled=True)  861 us
    all_gather x1, waiting for transfers between devices, local_block(): a_rows = lax.all_gather(a_block, 'co', axis=1, tiled=True)  121 us
    dot_general x1, matrix products, local_block(): product = jnp.dot(a_rows, b_cols, preferred_element_type=jnp.float32)  90.3 us
  transfers between devices with their start and end apart: 2, of which 2 were waited for; matrix products, arithmetic and copies ran while one was open for 0% of the time, Pallas kernels for 0%

commit v1 on v0

v1 whole, which is shorter than its diff:
```python
import functools

import jax
import jax.numpy as jnp
from jax import lax
from jax.experimental import pallas as pl
from jax.experimental.pallas import tpu as pltpu
from jax.sharding import PartitionSpec as P

MESH = pl.DeviceIdType.MESH
NT = 6
F32 = jnp.float32


def kernel(
    ny, nx, a_ref, b_ref, c_ref, bx, s1, ra,
    af, bt, sa, sb, rb, rc, rat, ct,
    bx_send, bx_recv, bt_sem, s1_send, s1_recv, s2_send, s2_recv, s3_send, s3_recv, s4_send, s4_recv,
    a_send, a_recv, b_send, b_recv, c_send, c_recv, ra_sem, ct_sem,
):
    y, x, core = lax.axis_index("ri"), lax.axis_index("co"), lax.axis_index("ro")
    rows = a_ref.shape[0]
    kh = b_ref.shape[0]
    w = b_ref.shape[1] // (2 * NT)
    q = rows // nx
    hq = q // 2

    def ym(d):
        return lax.rem(y + d + ny, ny)

    def xm(d):
        return lax.rem(x + d + nx, nx)

    def quarter(i):
        return pl.ds(pl.multiple_of(i * q, q), q)

    def rcopy(src, dst, ss, rs, **dev):
        return pltpu.make_async_remote_copy(
            src_ref=src, dst_ref=dst, send_sem=ss, recv_sem=rs, device_id=dev, device_id_type=MESH
        )

    barrier = pltpu.get_barrier_semaphore()
    for d in range(1, nx):
        pl.semaphore_signal(barrier, inc=1, device_id={"co": xm(d)}, device_id_type=MESH)
    for d in range(1, ny):
        pl.semaphore_signal(barrier, inc=1, device_id={"ri": ym(d)}, device_id_type=MESH)
    pl.semaphore_signal(barrier, inc=1, device_id={"ro": 1 - core}, device_id_type=MESH)
    pl.semaphore_wait(barrier, nx + ny - 1)

    def s1_copy(d):
        return rcopy(a_ref.at[quarter(xm(d))], s1.at[x], s1_send.at[d], s1_recv.at[x], co=xm(d))

    def s1_start():
        for d in (2, 1, 3):
            s1_copy(d).start()

    odd = lax.rem(x + y, 2) == 1

    @pl.when(odd)
    def _():
        s1_start()

    def cols(tile):
        return pl.ds(pl.multiple_of(tile * w, w), w)

    def bx_copy(tile):
        return rcopy(b_ref.at[:, cols(tile)], bx.at[:, cols(tile)], bx_send.at[tile], bx_recv.at[tile], ro=1 - core)

    def tile_a(t):
        return (1 - lax.rem(t, 2)) * NT + t // 2

    def tile_b(t):
        return lax.rem(t, 2) * NT + t // 2

    def bx_start(t, _):
        bx_copy(tile_a(t)).start()
        return 0

    lax.fori_loop(0, 2 * NT, bx_start, 0)

    def bt_copies(tile, slot):
        return (
            pltpu.make_async_copy(
                b_ref.at[:, cols(tile)], bt.at[slot, pl.ds(pl.multiple_of(core * kh, kh), kh)], bt_sem.at[slot, 0]
            ),
            pltpu.make_async_copy(
                bx.at[:, cols(tile)], bt.at[slot, pl.ds(pl.multiple_of((1 - core) * kh, kh), kh)], bt_sem.at[slot, 1]
            ),
        )

    def bt_start(tile, slot):
        for cp in bt_copies(tile, slot):
            cp.start()

    def bt_wait(tile, slot):
        for cp in bt_copies(tile, slot):
            cp.wait()

    def s2_piece(r, start):
        a = ym(r)
        here = a == x
        for src, cond in ((a_ref.at[quarter(x)], here), (s1.at[a], jnp.logical_not(here))):

            @pl.when(cond)
            def _(src=src):
                dst = af.at[y, quarter(x)]
                if r == 0:
                    cp = pltpu.make_async_copy(src, dst, s2_send.at[0])
                else:
                    cp = rcopy(src, dst, s2_send.at[r], s2_recv.at[y], ri=a)
                if start:
                    cp.start()
                elif r == 0:
                    cp.wait()
                else:
                    cp.wait_send()

    def s1_wait(r):
        a = ym(r)

        @pl.when(a != x)
        def _():
            rcopy(s1.at[a], s1.at[a], s1_send.at[0], s1_recv.at[a], co=a).wait_recv()

    def s2_wait(m):
        rcopy(af.at[m, quarter(x)], af.at[m, quarter(x)], s2_send.at[1], s2_recv.at[m], ri=m).wait_recv()

    def s3_copy(m, side):
        return rcopy(
            af.at[m, quarter(x)], af.at[m, quarter(x)], s3_send.at[m, side], s3_recv.at[m, side], co=xm(1 - 2 * side)
        )

    def half(i, side):
        return pl.ds(pl.multiple_of(i * q + side * hq, hq), hq)

    def s4_copy(m, side):
        part = af.at[m, half(xm(2 * side - 1), side)]
        return rcopy(part, part, s4_send.at[m, side], s4_recv.at[m, side], co=xm(1 - 2 * side))

    def s3_start(m):
        for side in range(2):
            s3_copy(m, side).start()

    def s3_recv_and_relay(m):
        for side in range(2):
            part = af.at[m, quarter(xm(2 * side - 1))]
            rcopy(part, part, s3_send.at[m, side], s3_recv.at[m, side], co=x).wait_recv()
            s4_copy(m, side).start()

    def s4_wait(m):
        for side in range(2):
            part = af.at[m, half(xm(2), side)]
            rcopy(part, part, s4_send.at[m, side], s4_recv.at[m, side], co=x).wait_recv()

    for r in (1, ny - 1):
        s1_wait(r)
        s2_piece(r, True)

    @pl.when(x == ym(2))
    def _():
        s1_start()

    for t in range(2):
        bx_copy(tile_a(t)).wait_recv()
    bt_start(tile_a(0), 0)
    for d in (1, ny - 1):
        s2_wait(ym(d))
        s3_start(ym(d))

    @pl.when(x == y)
    def _():
        s1_start()

    def dest(d):
        return lax.rem(y + 1 + d * (ny - 2), ny)

    def a_copy(d, k, i):
        return rcopy(
            sa.at[d, k, quarter(i)], ra.at[d, k, quarter(i)], a_send.at[d, k, i], a_recv.at[d, k, i], ri=dest(d)
        )

    def b_copy(d, k):
        return rcopy(sb.at[d, k], rb.at[d, k], b_send.at[d, k], b_recv.at[d, k], ri=dest(d))

    def c_copy(d, k):
        return rcopy(sa.at[d, k], rc.at[d, k], c_send.at[d, k], c_recv.at[d, k], ri=dest(d))

    last = 2 * NT - 1

    def run(this, nxt, work, before_next=None):
        def step(t, carry):
            slot = lax.rem(t, 2)

            @pl.when(t < last)
            def _():
                if before_next is not None:
                    before_next(t + 1)
                bt_start(this(t + 1), 1 - slot)

            if nxt is not None:

                @pl.when(t == last)
                def _():
                    bt_start(nxt(0), 1 - slot)

            bt_wait(this(t), slot)
            work(t, lax.rem(t, 2), t // 2, slot)
            return carry

        lax.fori_loop(0, 2 * NT, step, 0)

    def quarter_pass(j, nxt, before_next=None):
        i = xm(j)

        def work(t, d, k, slot):
            sa[d, k, quarter(i)] = jnp.dot(af[dest(d), quarter(i)], bt[slot], preferred_element_type=F32)
            a_copy(d, k, i).start()

        run(tile_a, nxt, work, before_next)

    def wait_bx(t):
        @pl.when(t >= 2)
        def _():
            bx_copy(tile_a(t)).wait_recv()

    quarter_pass(0, tile_a, wait_bx)
    s1_wait(2)
    s2_piece(2, True)
    for d in (1, ny - 1):
        s3_recv_and_relay(ym(d))
    quarter_pass(1, tile_a)
    s2_wait(ym(2))
    s3_start(ym(2))
    s1_wait(0)
    s2_piece(0, True)
    quarter_pass(nx - 1, tile_a)
    for d in (1, ny - 1):
        s4_wait(ym(d))
    s2_piece(0, False)
    s3_start(y)
    s3_recv_and_relay(ym(2))
    quarter_pass(2, tile_b)
    s4_wait(ym(2))
    s3_recv_and_relay(y)

    def b_work(t, d, k, slot):
        sb[d, k] = jnp.dot(af[ym(2)], bt[slot], preferred_element_type=F32)
        b_copy(d, k).start()

    run(tile_b, tile_b, b_work)
    s4_wait(y)

    def c_work(t, d, k, slot):
        for i in range(nx):
            a_copy(d, k, i).wait_send()
        b_copy(d, k).wait_recv()
        sa[d, k] = jnp.dot(af[dest(d)], bt[slot], preferred_element_type=F32) + rb[d, k]
        c_copy(d, k).start()

    run(tile_b, tile_b, c_work)

    def ra_copy(d, k, slot):
        return pltpu.make_async_copy(ra.at[1 - d, k], rat.at[slot], ra_sem.at[slot])

    def ra_start(d, k, slot):
        for i in range(nx):
            a_copy(1 - d, k, i).wait_recv()
        ra_copy(d, k, slot).start()

    def ct_copy(d, k, slot):
        return pltpu.make_async_copy(ct.at[slot], c_ref.at[:, cols(d * NT + k)], ct_sem.at[slot])

    ra_start(0, 0, 0)

    def own_work(t, d, k, slot):
        @pl.when(t < last)
        def _():
            ra_start(1 - d, (t + 1) // 2, 1 - slot)

        ra_copy(d, k, slot).wait()
        mine = jnp.dot(af[y], bt[slot], preferred_element_type=F32) + rat[slot]
        rat[slot] = mine
        c_copy(d, k).wait_recv()

        @pl.when(t >= 2)
        def _():
            ct_copy(d, k, slot).wait()

        ct[slot] = (rat[slot] + rc[d, k]).astype(ct.dtype)
        ct_copy(d, k, slot).start()

    run(tile_b, None, own_work)
    for d in range(2):
        ct_copy(d, NT - 1, d).wait()

    for d in (1, 2, 3):
        s1_copy(d).wait_send()
    for r in range(1, ny):
        s2_piece(r, False)
    for m in range(ny):
        for side in range(2):
            s3_copy(m, side).wait_send()
            s4_copy(m, side).wait_send()

    def drain(t, _):
        bx_copy(t).wait_send()
        b_copy(lax.rem(t, 2), t // 2).wait_send()
        c_copy(lax.rem(t, 2), t // 2).wait_send()
        return 0

    lax.fori_loop(0, 2 * NT, drain, 0)


def solution(mesh):
    grid_spec = P(("dp", "ri", "ro"), "co")
    ny, nx = mesh.shape["ri"], mesh.shape["co"]

    def local_block(a, b):
        rows, depth = a.shape
        kh, width = b.shape
        w = width // (2 * NT)
        q = rows // nx
        any_spec = pl.BlockSpec(memory_space=pl.ANY)
        dma = pltpu.SemaphoreType.DMA
        out = pl.pallas_call(
            functools.partial(kernel, ny, nx),
            out_shape=[
                jax.ShapeDtypeStruct((rows, width), jnp.bfloat16),
                jax.ShapeDtypeStruct((kh, width), b.dtype),
                jax.ShapeDtypeStruct((nx, q, depth), a.dtype),
                jax.ShapeDtypeStruct((2, NT, rows, w), F32),
            ],
            in_specs=[any_spec] * 2,
            out_specs=[any_spec] * 4,
            scratch_shapes=[
                pltpu.VMEM((ny, rows, depth), a.dtype),
                pltpu.VMEM((2, 2 * kh, w), b.dtype),
                pltpu.VMEM((2, NT, rows, w), F32),
                pltpu.VMEM((2, NT, rows, w), F32),
                pltpu.VMEM((2, NT, rows, w), F32),
                pltpu.VMEM((2, NT, rows, w), F32),
                pltpu.VMEM((2, rows, w), F32),
                pltpu.VMEM((2, rows, w), jnp.bfloat16),
                dma((2 * NT,)), dma((2 * NT,)), dma((2, 2)),
                dma((nx,)), dma((nx,)), dma((ny,)), dma((ny,)),
                dma((ny, 2)), dma((ny, 2)), dma((ny, 2)), dma((ny, 2)),
                dma((2, NT, nx)), dma((2, NT, nx)),
                dma((2, NT)), dma((2, NT)), dma((2, NT)), dma((2, NT)),
                dma((2,)), dma((2,)),
            ],
            compiler_params=pltpu.CompilerParams(
                collective_id=0, has_side_effects=True, vmem_limit_bytes=67043328
            ),
        )(a, b)
        return out[0]

    return jax.shard_map(local_block, mesh=mesh, in_specs=(grid_spec, grid_spec), out_specs=grid_spec, check_vma=False)
```

time: 1090 us -> 401 us (0.37)
  waiting for transfers between devices: 984 us -> 0 us
  Pallas kernels: 0 us -> 395 us
  matrix products: 90.3 us -> 0 us
  between operations: 13.4 us -> 0.01 us
    all_gather x2 -> x0, waiting for transfers between devices: 983 us -> none  [the longest x1 861 us: local_block(): b_cols = lax.all_gather(b_block, ('ri', 'ro'), axis=0, tiled=True)]
    pallas_call x0 -> x1, Pallas kernels: none -> 395 us  [local_block(): pl.pallas_call(functools.partial(kernel, ny, nx), out_shape=[jax.ShapeDty...]
    dot_general x1 -> x0, matrix products: 90.3 us -> none  [local_block(): product = jnp.dot(a_rows, b_cols, preferred_element_type=jnp.float32)]
  transfers between devices with their start and end apart: 2 -> 0, of which waited for: 2 -> 0; matrix products, arithmetic and copies ran while one was open for 0% -> 0% of each run, Pallas kernels for 0% -> 0%
where the time goes in v1:
time: 401 us; the launch traced here: 400 us
  Pallas kernels  395 us (99%)
  local copies, waits for them, and re-layouts  5.05 us (1%)
    pallas_call x1, Pallas kernels, local_block(): pl.pallas_call(functools.partial(kernel, ny, nx), out_shape=[jax.ShapeDty...  395 us

profile of v1, /device:TPU:97, one launch (start us, length us, event | category | flops | bytes accessed | tf_op | source)
XLA Modules:
  0.0 400.4 jit_solution(9518391182496132229)
XLA Ops:
  0.0 395.3 %shard_map.28 = (bf16[384,6144]{1,0:T(8,128)(2,1)}, bf16[2048,6144]{1,0:T(8,128)(2,1)}, bf16[4,96,4096]{2,1,0:T(8,128)(2,1)}, f32[2,6,384,512]{3,2,1,0:T(8,128)}) custom-call(bf16[384,4096]{1,0:T(8,128)(2,1)} %a_ref.1, bf16[2048,6144]{1,0:T(8,128)(2,1)} %b_ref.1), custom_call_target="tpu_custom_call" | custom-call | tf_op jit(solution)/shard_map/pallas_call | solution.py:325
  395.3 5.1 %copy.4 = bf16[384,6144]{1,0:T(8,128)(2,1)} copy(bf16[384,6144]{1,0:T(8,128)(2,1)} %get-tuple-element.6) | data formatting | bytes 9437184

commit v2 on v0

v2 whole, which is shorter than its diff:
```python
import functools

import jax
import jax.numpy as jnp
from jax import lax
from jax.experimental import pallas as pl
from jax.experimental.pallas import tpu as pltpu
from jax.sharding import PartitionSpec as P

MESH = pl.DeviceIdType.MESH
NT = 6
F32 = jnp.float32


def kernel(
    ny, nx, a_ref, b_ref, c_ref, bx, s1, f1, f2, ra,
    af, bt, sa, sb, rb, rc, rat, ct,
    bx_send, bx_recv, bt_sem, s1_send, s1_recv, d2_send, f1_send, f1_recv, s2_send, s2_recv, own_sem,
    s2b_send, f2_send, f2_recv, s3_send, s3_recv, s4_send, s4_recv,
    a_send, a_recv, b_send, b_recv, c_send, c_recv, ra_sem, ct_sem,
):
    y, x, core = lax.axis_index("ri"), lax.axis_index("co"), lax.axis_index("ro")
    rows = a_ref.shape[0]
    kh = b_ref.shape[0]
    w = b_ref.shape[1] // (2 * NT)
    q = rows // nx
    u = q // 3
    h = u // 2
    tiles = 2 * NT

    SUB = ((0, u), (u, 2 * u))
    A_ROWS = ((0, u), (u, 2 * u), (3 * u, 2 * u), (5 * u, 4 * u), (9 * u, 3 * u))
    B_ROWS = ((0, 3 * u), (3 * u, 9 * u))
    S3_AT = ((4 * u, 7 * u), (3 * u, 5 * u))
    S4 = ((0, 7 * u, 10 * u, 3 * h), (1, 3 * u, 9 * u, u), (1, 13 * h, 23 * h, h))
    OUT = ((0, 0, 0, 3 * u), (1, 0, 3 * u, u), (nx - 1, 0, 4 * u, u), (1, u, 5 * u, 2 * u),
           (nx - 1, u, 7 * u, 2 * u), (2, 0, 9 * u, 3 * u))

    def ym(d):
        return lax.rem(y + d + ny, ny)

    def xm(d):
        return lax.rem(x + d + nx, nx)

    def at_quarter(i, first, n):
        return pl.ds(pl.multiple_of(i * q + first, h), n)

    def rcopy(src, dst, ss, rs, **dev):
        return pltpu.make_async_remote_copy(
            src_ref=src, dst_ref=dst, send_sem=ss, recv_sem=rs, device_id=dev, device_id_type=MESH
        )

    barrier = pltpu.get_barrier_semaphore()
    for d in (1, nx - 1):
        pl.semaphore_signal(barrier, inc=1, device_id={"co": xm(d)}, device_id_type=MESH)
    for d in (1, ny - 1):
        pl.semaphore_signal(barrier, inc=1, device_id={"ri": ym(d)}, device_id_type=MESH)
    pl.semaphore_signal(barrier, inc=1, device_id={"ro": 1 - core}, device_id_type=MESH)
    pl.semaphore_wait(barrier, 5)

    odd = lax.rem(x + y, 2) == 1
    even = jnp.logical_not(odd)

    def split(piece, side):
        first, n = SUB[piece]
        return first + side * (n // 2), n // 2

    def f1_rows(piece):
        return pl.ds(piece * h, (piece + 1) * h)

    def d1_copy(side, piece):
        first, n = SUB[piece]
        return rcopy(
            a_ref.at[at_quarter(xm(1 - 2 * side), first, n)], s1.at[x, pl.ds(first, n)],
            s1_send.at[side, piece], s1_recv.at[x, piece, 0], co=xm(1 - 2 * side),
        )

    def d2_copy(side, piece):
        first, n = split(piece, side)
        return rcopy(
            a_ref.at[at_quarter(xm(2), first, n)], f1.at[side, f1_rows(piece)],
            d2_send.at[side, piece], f1_recv.at[side, piece], co=xm(1 - 2 * side),
        )

    def f1_copy(side, piece):
        first, n = split(piece, side)
        source = xm(2 * side - 1)
        return rcopy(
            f1.at[side, f1_rows(piece)], s1.at[source, pl.ds(first, n)],
            f1_send.at[side, piece], s1_recv.at[source, piece, side], co=xm(1 - 2 * side),
        )

    def s1_start():
        for piece in range(2):
            for make in (d2_copy, d1_copy):
                for side in range(2):
                    make(side, piece).start()

    def f1_relay(piece):
        for side in range(2):
            d2_copy(side, piece).wait_recv()
            f1_copy(side, piece).start()

    def s1_wait(r, piece):
        a = ym(r)

        @pl.when(lax.rem(a + x, 2) == 1)
        def _():
            first, n = SUB[piece]
            part = s1.at[a, pl.ds(first, n)]
            rcopy(part, part, s1_send.at[0, 0], s1_recv.at[a, piece, 0], co=x).wait_recv()

        @pl.when(a == xm(2))
        def _():
            for side in range(2):
                first, n = split(piece, side)
                part = s1.at[a, pl.ds(first, n)]
                rcopy(part, part, s1_send.at[0, 0], s1_recv.at[a, piece, side], co=x).wait_recv()

    def cols(tile):
        return pl.ds(pl.multiple_of(tile * w, w), w)

    def bx_copy(tile):
        return rcopy(b_ref.at[:, cols(tile)], bx.at[:, cols(tile)], bx_send.at[tile], bx_recv.at[tile], ro=1 - core)

    def tile_a(t):
        return (1 - lax.rem(t, 2)) * NT + t // 2

    def tile_b(t):
        return lax.rem(t, 2) * NT + t // 2

    def bt_copies(tile, slot):
        return (
            pltpu.make_async_copy(
                b_ref.at[:, cols(tile)], bt.at[slot, pl.ds(pl.multiple_of(core * kh, kh), kh)], bt_sem.at[slot, 0]
            ),
            pltpu.make_async_copy(
                bx.at[:, cols(tile)], bt.at[slot, pl.ds(pl.multiple_of((1 - core) * kh, kh), kh)], bt_sem.at[slot, 1]
            ),
        )

    def bt_start(tile, slot):
        for cp in bt_copies(tile, slot):
            cp.start()

    def bt_wait(tile, slot):
        for cp in bt_copies(tile, slot):
            cp.wait()

    def from_a(a, first, n, do):
        for src, cond in ((a_ref.at[at_quarter(x, first, n)], a == x), (s1.at[a, pl.ds(first, n)], a != x)):

            @pl.when(cond)
            def _(src=src):
                do(src)

    def s2_copy(r, piece, src):
        first, n = SUB[piece]
        return rcopy(src, af.at[y, pl.ds(first, n)], s2_send.at[r, piece], s2_recv.at[y, piece], ri=ym(r))

    def s2_wait(m, piece):
        first, n = SUB[piece]
        part = af.at[m, pl.ds(first, n)]
        rcopy(part, part, s2_send.at[1, 0], s2_recv.at[m, piece], ri=y).wait_recv()

    def s2_early(r):
        @pl.when(ym(r) == x)
        def _():
            for piece in range(2):
                first, n = SUB[piece]
                s2_copy(r, piece, a_ref.at[at_quarter(x, first, n)]).start()

    def s2_start(r, piece):
        s1_wait(r, piece)

        @pl.when(ym(r) != x)
        def _():
            first, n = SUB[piece]
            s2_copy(r, piece, s1.at[ym(r), pl.ds(first, n)]).start()

    def s2b_start():
        for side in range(2):
            from_a(
                ym(2), side * 3 * h, 3 * h,
                lambda src, side=side: rcopy(
                    src, f2.at[side], s2b_send.at[side], f2_recv.at[side], ri=ym(1 - 2 * side)
                ).start(),
            )

    def f2_copy(side):
        m = ym(2 * side - 1)
        return rcopy(
            f2.at[side], af.at[m, pl.ds(side * 3 * h, 3 * h)], f2_send.at[side], s2_recv.at[m, side], ri=ym(1 - 2 * side)
        )

    def f2_relay():
        for side in range(2):
            rcopy(f2.at[side], f2.at[side], s2b_send.at[side], f2_recv.at[side], ri=y).wait_recv()
            f2_copy(side).start()

    def f2_wait():
        m = ym(2)
        for side in range(2):
            part = af.at[m, pl.ds(side * 3 * h, 3 * h)]
            rcopy(part, part, f2_send.at[side], s2_recv.at[m, side], ri=y).wait_recv()

    def own_copy(src):
        return pltpu.make_async_copy(src, af.at[y, pl.ds(0, q)], own_sem)

    def s3_copy(m, side, piece):
        first, n = SUB[piece]
        return rcopy(
            af.at[m, pl.ds(first, n)], af.at[m, pl.ds(S3_AT[side][piece], n)],
            s3_send.at[m, side, piece], s3_recv.at[m, side, piece], co=xm(1 - 2 * side),
        )

    def s3_start(m, piece):
        for side in range(2):
            s3_copy(m, side, piece).start()

    def s3_wait(m, piece):
        for side in range(2):
            s3_copy(m, side, piece).wait_recv()

    def s4_copy(m, i):
        side, src, dst, n = S4[i]
        return rcopy(
            af.at[m, pl.ds(src, n)], af.at[m, pl.ds(dst, n)], s4_send.at[m, i], s4_recv.at[m, i], co=xm(1 - 2 * side)
        )

    def s4_start(m):
        for i in range(3):
            s4_copy(m, i).start()

    def s4_wait(m):
        for i in range(3):
            s4_copy(m, i).wait_recv()

    near = (1, ny - 1)

    @pl.when(odd)
    def _():
        s1_start()

    for r in near:
        s2_early(r)

    def bx_start(t, _):
        bx_copy(tile_a(t)).start()
        return 0

    lax.fori_loop(0, tiles, bx_start, 0)

    @pl.when(even)
    def _():
        f1_relay(0)

    for r in near:
        s2_start(r, 0)

    @pl.when(even)
    def _():
        f1_relay(1)
        s1_start()

    for t in range(2):
        bx_copy(tile_a(t)).wait_recv()
        bt_start(tile_a(t), t)
    for r in near:
        s2_wait(ym(r), 0)
        s3_start(ym(r), 0)

    def dest(d):
        return lax.rem(y + 1 + d * (ny - 2), ny)

    def a_copy(d, k, i):
        part = pl.ds(*A_ROWS[i])
        return rcopy(sa.at[d, k, part], ra.at[d, k, part], a_send.at[d, k, i], a_recv.at[d, k, i], ri=dest(d))

    def b_copy(d, k, i):
        part = pl.ds(*B_ROWS[i])
        return rcopy(sb.at[d, k, part], rb.at[d, k, part], b_send.at[d, k, i], b_recv.at[d, k, i], ri=dest(d))

    def c_copy(d, k):
        return rcopy(sa.at[d, k], rc.at[d, k], c_send.at[d, k], c_recv.at[d, k], ri=dest(d))

    def run(this, nxt, work, each=None):
        def step(t, carry):
            if each is not None:
                each(t)

            @pl.when(t + 2 < tiles)
            def _():
                bt_start(this(t + 2), lax.rem(t + 2, 3))

            if nxt is not None:

                @pl.when(t + 2 >= tiles)
                def _():
                    bt_start(nxt(t + 2 - tiles), lax.rem(t + 2, 3))

            slot = lax.rem(t, 3)
            bt_wait(this(t), slot)
            work(t, lax.rem(t, 2), t // 2, slot)
            return carry

        lax.fori_loop(0, tiles, step, 0)

    def a_pass(i, nxt, each=None):
        part = pl.ds(*A_ROWS[i])

        def work(t, d, k, slot):
            sa[d, k, part] = jnp.dot(af[dest(d), part], bt[slot], preferred_element_type=F32)
            a_copy(d, k, i).start()

        run(tile_a, nxt, work, each)

    def first_pass(t):
        @pl.when(t + 2 < tiles)
        def _():
            bx_copy(tile_a(t + 2)).wait_recv()

        @pl.when(t == NT)
        def _():
            for r in near:
                s2_start(r, 1)

    a_pass(0, tile_a, first_pass)
    for r in near:
        s2_wait(ym(r), 1)
        s3_start(ym(r), 1)
    a_pass(1, tile_a)

    @pl.when(odd)
    def _():
        f1_relay(0)
        f1_relay(1)

    for r in near:
        s3_wait(ym(r), 0)
    a_pass(2, tile_a)
    for piece in range(2):
        s1_wait(2, piece)
    s2b_start()
    for r in near:
        s3_wait(ym(r), 1)
        s4_start(ym(r))
    a_pass(3, tile_a)
    f2_relay()
    for r in near:
        s4_wait(ym(r))
    a_pass(4, tile_b)
    f2_wait()
    for piece in range(2):
        s3_start(ym(2), piece)
        s1_wait(0, piece)
    from_a(y, 0, q, lambda src: own_copy(src).start())

    def b_pass(i, nxt):
        part = pl.ds(*B_ROWS[i])

        def work(t, d, k, slot):
            sb[d, k, part] = jnp.dot(af[ym(2), part], bt[slot], preferred_element_type=F32)
            b_copy(d, k, i).start()

        run(tile_b, nxt, work)

    b_pass(0, tile_b)
    for piece in range(2):
        s3_wait(ym(2), piece)
    s4_start(ym(2))
    from_a(y, 0, q, lambda src: own_copy(src).wait())
    for piece in range(2):
        s3_start(y, piece)
    s4_wait(ym(2))
    b_pass(1, tile_b)
    for piece in range(2):
        s3_wait(y, piece)
    s4_start(y)

    def c_work(t, d, k, slot):
        for i in range(len(A_ROWS)):
            a_copy(d, k, i).wait_send()
        for i in range(len(B_ROWS)):
            b_copy(d, k, i).wait_recv()
        sa[d, k] = jnp.dot(af[dest(d)], bt[slot], preferred_element_type=F32) + rb[d, k]
        c_copy(d, k).start()

    run(tile_b, tile_b, c_work)
    s4_wait(y)

    def ra_copy(d, k, slot):
        return pltpu.make_async_copy(ra.at[1 - d, k], rat.at[slot], ra_sem.at[slot])

    def ra_start(d, k, slot):
        for i in range(len(A_ROWS)):
            a_copy(1 - d, k, i).wait_recv()
        ra_copy(d, k, slot).start()

    def ct_copies(d, k, slot):
        return [
            pltpu.make_async_copy(
                ct.at[slot, pl.ds(src, n)], c_ref.at[at_quarter(xm(j), first, n), cols(d * NT + k)], ct_sem.at[slot, i]
            )
            for i, (j, first, src, n) in enumerate(OUT)
        ]

    ra_start(0, 0, 0)

    def own_work(t, d, k, slot):
        @pl.when(t < tiles - 1)
        def _():
            ra_start(1 - d, (t + 1) // 2, 1 - d)

        ra_copy(d, k, d).wait()
        rat[d] = jnp.dot(af[y], bt[slot], preferred_element_type=F32) + rat[d]
        c_copy(d, k).wait_recv()

        @pl.when(t >= 2)
        def _():
            for cp in ct_copies(d, k, d):
                cp.wait()

        ct[d] = (rat[d] + rc[d, k]).astype(ct.dtype)
        for cp in ct_copies(d, k, d):
            cp.start()

    run(tile_b, None, own_work)
    for d in range(2):
        for cp in ct_copies(d, NT - 1, d):
            cp.wait()

    for side in range(2):
        for piece in range(2):
            for make in (d1_copy, d2_copy, f1_copy):
                make(side, piece).wait_send()
        rcopy(f2.at[side], f2.at[side], s2b_send.at[side], f2_recv.at[side], ri=y).wait_send()
        f2_copy(side).wait_send()
    for piece in range(2):
        for r in near:
            first, n = SUB[piece]
            s2_copy(r, piece, s1.at[y, pl.ds(first, n)]).wait_send()
    for m in range(ny):
        for side in range(2):
            for piece in range(2):
                s3_copy(m, side, piece).wait_send()
        for i in range(3):
            s4_copy(m, i).wait_send()

    def drain(t, _):
        d, k = lax.rem(t, 2), t // 2
        bx_copy(t).wait_send()
        for i in range(len(B_ROWS)):
            b_copy(d, k, i).wait_send()
        c_copy(d, k).wait_send()
        return 0

    lax.fori_loop(0, tiles, drain, 0)


def solution(mesh):
    grid_spec = P(("dp", "ri", "ro"), "co")
    ny, nx = mesh.shape["ri"], mesh.shape["co"]

    def local_block(a, b):
        rows, depth = a.shape
        kh, width = b.shape
        w = width // (2 * NT)
        q = rows // nx
        any_spec = pl.BlockSpec(memory_space=pl.ANY)
        dma = pltpu.SemaphoreType.DMA
        out = pl.pallas_call(
            functools.partial(kernel, ny, nx),
            out_shape=[
                jax.ShapeDtypeStruct((rows, width), jnp.bfloat16),
                jax.ShapeDtypeStruct((kh, width), b.dtype),
                jax.ShapeDtypeStruct((nx, q, depth), a.dtype),
                jax.ShapeDtypeStruct((2, q // 2, depth), a.dtype),
                jax.ShapeDtypeStruct((2, q // 2, depth), a.dtype),
                jax.ShapeDtypeStruct((2, NT, rows, w), F32),
            ],
            in_specs=[any_spec] * 2,
            out_specs=[any_spec] * 6,
            scratch_shapes=[
                pltpu.VMEM((ny, rows, depth), a.dtype),
                pltpu.VMEM((3, 2 * kh, w), b.dtype),
                pltpu.VMEM((2, NT, rows, w), F32),
                pltpu.VMEM((2, NT, rows, w), F32),
                pltpu.VMEM((2, NT, rows, w), F32),
                pltpu.VMEM((2, NT, rows, w), F32),
                pltpu.VMEM((2, rows, w), F32),
                pltpu.VMEM((2, rows, w), jnp.bfloat16),
                dma((2 * NT,)), dma((2 * NT,)), dma((3, 2)),
                dma((2, 2)), dma((nx, 2, 2)), dma((2, 2)), dma((2, 2)), dma((2, 2)), dma((ny, 2)), dma((ny, 2)), dma,
                dma((2,)), dma((2,)), dma((2,)), dma((ny, 2, 2)), dma((ny, 2, 2)), dma((ny, 3)), dma((ny, 3)),
                dma((2, NT, 5)), dma((2, NT, 5)), dma((2, NT, 2)), dma((2, NT, 2)), dma((2, NT)), dma((2, NT)),
                dma((2,)), dma((2, 6)),
            ],
            compiler_params=pltpu.CompilerParams(
                collective_id=0, has_side_effects=True, vmem_limit_bytes=67043328
            ),
        )(a, b)
        return out[0]

    return jax.shard_map(local_block, mesh=mesh, in_specs=(grid_spec, grid_spec), out_specs=grid_spec, check_vma=False)
```

time: 1090 us -> 374 us (0.34)
  waiting for transfers between devices: 984 us -> 0 us
  Pallas kernels: 0 us -> 367 us
  matrix products: 90.3 us -> 0 us
  between operations: 13.4 us -> 0.01 us
    all_gather x2 -> x0, waiting for transfers between devices: 983 us -> none  [the longest x1 861 us: local_block(): b_cols = lax.all_gather(b_block, ('ri', 'ro'), axis=0, tiled=True)]
    pallas_call x0 -> x1, Pallas kernels: none -> 367 us  [local_block(): pl.pallas_call(functools.partial(kernel, ny, nx), out_shape=[jax.ShapeDty...]
    dot_general x1 -> x0, matrix products: 90.3 us -> none  [local_block(): product = jnp.dot(a_rows, b_cols, preferred_element_type=jnp.float32)]
  transfers between devices with their start and end apart: 2 -> 0, of which waited for: 2 -> 0; matrix products, arithmetic and copies ran while one was open for 0% -> 0% of each run, Pallas kernels for 0% -> 0%
where the time goes in v2:
time: 374 us; the launch traced here: 372 us
  Pallas kernels  367 us (98%)
  local copies, waits for them, and re-layouts  5.05 us (1%)
    pallas_call x1, Pallas kernels, local_block(): pl.pallas_call(functools.partial(kernel, ny, nx), out_shape=[jax.ShapeDty...  367 us

profile of v2, /device:TPU:97, one launch (start us, length us, event | category | flops | bytes accessed | tf_op | source)
XLA Modules:
  0.0 372.2 jit_solution(3861351272995355553)
XLA Ops:
  0.0 367.1 %shard_map.28 = (bf16[384,6144]{1,0:T(8,128)(2,1)}, bf16[2048,6144]{1,0:T(8,128)(2,1)}, bf16[4,96,4096]{2,1,0:T(8,128)(2,1)}, bf16[2,48,4096]{2,1,0:T(8,128)(2,1...) custom-call(bf16[384,4096]{1,0:T(8,128)(2,1)} %a_ref.1, bf16[2048,6144]{1,0:T(8,128)(2,1)} %b_ref.1), custom_call_target="tpu_custom_call" | custom-call | tf_op jit(solution)/shard_map/pallas_call | solution.py:472
  367.1 5.1 %copy.4 = bf16[384,6144]{1,0:T(8,128)(2,1)} copy(bf16[384,6144]{1,0:T(8,128)(2,1)} %get-tuple-element.6) | data formatting | bytes 9437184

commit v3 on v2

--- a/solution.py
+++ b/solution.py
@@ -9,6 +9,7 @@
 
 MESH = pl.DeviceIdType.MESH
 NT = 6
+KC = 4
 F32 = jnp.float32
 
 
@@ -24,17 +25,20 @@
     kh = b_ref.shape[0]
     w = b_ref.shape[1] // (2 * NT)
     q = rows // nx
-    u = q // 3
+    u = q // 2
     h = u // 2
+    kw = a_ref.shape[1] // KC
     tiles = 2 * NT
 
-    SUB = ((0, u), (u, 2 * u))
-    A_ROWS = ((0, u), (u, 2 * u), (3 * u, 2 * u), (5 * u, 4 * u), (9 * u, 3 * u))
-    B_ROWS = ((0, 3 * u), (3 * u, 9 * u))
-    S3_AT = ((4 * u, 7 * u), (3 * u, 5 * u))
-    S4 = ((0, 7 * u, 10 * u, 3 * h), (1, 3 * u, 9 * u, u), (1, 13 * h, 23 * h, h))
-    OUT = ((0, 0, 0, 3 * u), (1, 0, 3 * u, u), (nx - 1, 0, 4 * u, u), (1, u, 5 * u, 2 * u),
-           (nx - 1, u, 7 * u, 2 * u), (2, 0, 9 * u, 3 * u))
+    def sub(piece):
+        return pl.ds(piece * u, u)
+
+    A_ROWS = ((0, u), (u, u), (2 * u, 2 * u), (4 * u, 2 * u), (6 * u, 2 * u))
+    B_ROWS = ((0, 2 * u), (2 * u, 6 * u))
+    S3_AT = ((3 * u, 5 * u), (2 * u, 4 * u))
+    S4 = ((0, 5 * u, 7 * u), (1, 2 * u, 6 * u))
+    OUT = ((0, 0, 0, 2 * u), (1, 0, 2 * u, u), (nx - 1, 0, 3 * u, u), (1, u, 4 * u, u),
+           (nx - 1, u, 5 * u, u), (2, 0, 6 * u, 2 * u))
 
     def ym(d):
         return lax.rem(y + d + ny, ny)
@@ -61,61 +65,64 @@
     odd = lax.rem(x + y, 2) == 1
     even = jnp.logical_not(odd)
 
-    def split(piece, side):
-        first, n = SUB[piece]
-        return first + side * (n // 2), n // 2
-
-    def f1_rows(piece):
-        return pl.ds(piece * h, (piece + 1) * h)
-
-    def d1_copy(side, piece):
-        first, n = SUB[piece]
+    def piece_of(chunk):
+        return (1, slice(None)) if chunk == KC else (0, pl.ds(chunk * kw, kw))
+
+    def s1_part(a, chunk):
+        piece, at = piece_of(chunk)
+        return s1.at[a, sub(piece), at]
+
+    def s1_half(a, chunk, side):
+        piece, at = piece_of(chunk)
+        return s1.at[a, pl.ds(piece * u + side * h, h), at]
+
+    def f1_part(side, chunk):
+        piece, at = piece_of(chunk)
+        return f1.at[side, pl.ds(piece * h, h), at]
+
+    def d1_copy(side, chunk):
+        piece, at = piece_of(chunk)
         return rcopy(
-            a_ref.at[at_quarter(xm(1 - 2 * side), first, n)], s1.at[x, pl.ds(first, n)],
-            s1_send.at[side, piece], s1_recv.at[x, piece, 0], co=xm(1 - 2 * side),
-        )
-
-    def d2_copy(side, piece):
-        first, n = split(piece, side)
+            a_ref.at[at_quarter(xm(1 - 2 * side), piece * u, u), at], s1_part(x, chunk),
+            s1_send.at[side, chunk], s1_recv.at[x, chunk, 0], co=xm(1 - 2 * side),
+        )
+
+    def d2_copy(side, chunk):
+        piece, at = piece_of(chunk)
         return rcopy(
-            a_ref.at[at_quarter(xm(2), first, n)], f1.at[side, f1_rows(piece)],
-            d2_send.at[side, piece], f1_recv.at[side, piece], co=xm(1 - 2 * side),
-        )
-
-    def f1_copy(side, piece):
-        first, n = split(piece, side)
+            a_ref.at[at_quarter(xm(2), piece * u + side * h, h), at], f1_part(side, chunk),
+            d2_send.at[side, chunk], f1_recv.at[side, chunk], co=xm(1 - 2 * side),
+        )
+
+    def f1_copy(side, chunk):
         source = xm(2 * side - 1)
         return rcopy(
-            f1.at[side, f1_rows(piece)], s1.at[source, pl.ds(first, n)],
-            f1_send.at[side, piece], s1_recv.at[source, piece, side], co=xm(1 - 2 * side),
-        )
-
-    def s1_start():
-        for piece in range(2):
-            for make in (d2_copy, d1_copy):
-                for side in range(2):
-                    make(side, piece).start()
-
-    def f1_relay(piece):
-        for side in range(2):
-            d2_copy(side, piece).wait_recv()
-            f1_copy(side, piece).start()
-
-    def s1_wait(r, piece):
+            f1_part(side, chunk), s1_half(source, chunk, side),
+            f1_send.at[side, chunk], s1_recv.at[source, chunk, side], co=xm(1 - 2 * side),
+        )
+
+    def both(make, chunk):
+        for side in range(2):
+            make(side, chunk).start()
+
+    def f1_relay(chunk):
+        for side in range(2):
+            d2_copy(side, chunk).wait_recv()
+            f1_copy(side, chunk).start()
+
+    def s1_wait(r, chunk):
         a = ym(r)
 
         @pl.when(lax.rem(a + x, 2) == 1)
         def _():
-            first, n = SUB[piece]
-            part = s1.at[a, pl.ds(first, n)]
-            rcopy(part, part, s1_send.at[0, 0], s1_recv.at[a, piece, 0], co=x).wait_recv()
+            part = s1_part(a, chunk)
+            rcopy(part, part, s1_send.at[0, 0], s1_recv.at[a, chunk, 0], co=x).wait_recv()
 
         @pl.when(a == xm(2))
         def _():
             for side in range(2):
-                first, n = split(piece, side)
-                part = s1.at[a, pl.ds(first, n)]
-                rcopy(part, part, s1_send.at[0, 0], s1_recv.at[a, piece, side], co=x).wait_recv()
+                part = s1_half(a, chunk, side)
+                rcopy(part, part, s1_send.at[0, 0], s1_recv.at[a, chunk, side], co=x).wait_recv()
 
     def cols(tile):
         return pl.ds(pl.multiple_of(tile * w, w), w)
@@ -154,34 +161,33 @@
             def _(src=src):
                 do(src)
 
-    def s2_copy(r, piece, src):
-        first, n = SUB[piece]
-        return rcopy(src, af.at[y, pl.ds(first, n)], s2_send.at[r, piece], s2_recv.at[y, piece], ri=ym(r))
-
-    def s2_wait(m, piece):
-        first, n = SUB[piece]
-        part = af.at[m, pl.ds(first, n)]
-        rcopy(part, part, s2_send.at[1, 0], s2_recv.at[m, piece], ri=y).wait_recv()
+    def s2_copy(r, chunk, src):
+        piece, at = piece_of(chunk)
+        return rcopy(src, af.at[y, sub(piece), at], s2_send.at[r, chunk], s2_recv.at[y, chunk], ri=ym(r))
+
+    def s2_wait(m, chunk):
+        piece, at = piece_of(chunk)
+        part = af.at[m, sub(piece), at]
+        rcopy(part, part, s2_send.at[1, 0], s2_recv.at[m, chunk], ri=y).wait_recv()
 
     def s2_early(r):
         @pl.when(ym(r) == x)
         def _():
-            for piece in range(2):
-                first, n = SUB[piece]
-                s2_copy(r, piece, a_ref.at[at_quarter(x, first, n)]).start()
-
-    def s2_start(r, piece):
-        s1_wait(r, piece)
+            for chunk in range(KC + 1):
+                piece, at = piece_of(chunk)
+                s2_copy(r, chunk, a_ref.at[at_quarter(x, piece * u, u), at]).start()
+
+    def s2_start(r, chunk):
+        s1_wait(r, chunk)
 
         @pl.when(ym(r) != x)
         def _():
-            first, n = SUB[piece]
-            s2_copy(r, piece, s1.at[ym(r), pl.ds(first, n)]).start()
+            s2_copy(r, chunk, s1_part(ym(r), chunk)).start()
 
     def s2b_start():
         for side in range(2):
             from_a(
-                ym(2), side * 3 * h, 3 * h,
+                ym(2), side * u, u,
                 lambda src, side=side: rcopy(
                     src, f2.at[side], s2b_send.at[side], f2_recv.at[side], ri=ym(1 - 2 * side)
                 ).start(),
@@ -189,9 +195,7 @@
 
     def f2_copy(side):
         m = ym(2 * side - 1)
-        return rcopy(
-            f2.at[side], af.at[m, pl.ds(side * 3 * h, 3 * h)], f2_send.at[side], s2_recv.at[m, side], ri=ym(1 - 2 * side)
-        )
+        return rcopy(f2.at[side], af.at[m, sub(side)], f2_send.at[side], s2_recv.at[m, side], ri=ym(1 - 2 * side))
 
     def f2_relay():
         for side in range(2):
@@ -201,16 +205,15 @@
     def f2_wait():
         m = ym(2)
         for side in range(2):
-            part = af.at[m, pl.ds(side * 3 * h, 3 * h)]
+            part = af.at[m, sub(side)]
             rcopy(part, part, f2_send.at[side], s2_recv.at[m, side], ri=y).wait_recv()
 
     def own_copy(src):
         return pltpu.make_async_copy(src, af.at[y, pl.ds(0, q)], own_sem)
 
     def s3_copy(m, side, piece):
-        first, n = SUB[piece]
         return rcopy(
-            af.at[m, pl.ds(first, n)], af.at[m, pl.ds(S3_AT[side][piece], n)],
+            af.at[m, sub(piece)], af.at[m, pl.ds(S3_AT[side][piece], u)],
             s3_send.at[m, side, piece], s3_recv.at[m, side, piece], co=xm(1 - 2 * side),
         )
 
@@ -223,24 +226,31 @@
             s3_copy(m, side, piece).wait_recv()
 
     def s4_copy(m, i):
-        side, src, dst, n = S4[i]
+        side, src, dst = S4[i]
         return rcopy(
-            af.at[m, pl.ds(src, n)], af.at[m, pl.ds(dst, n)], s4_send.at[m, i], s4_recv.at[m, i], co=xm(1 - 2 * side)
+            af.at[m, pl.ds(src, u)], af.at[m, pl.ds(dst, u)], s4_send.at[m, i], s4_recv.at[m, i], co=xm(1 - 2 * side)
         )
 
     def s4_start(m):
-        for i in range(3):
+        for i in range(2):
             s4_copy(m, i).start()
 
     def s4_wait(m):
-        for i in range(3):
+        for i in range(2):
             s4_copy(m, i).wait_recv()
 
     near = (1, ny - 1)
 
     @pl.when(odd)
     def _():
-        s1_start()
+        for chunk in range(KC + 1):
+            both(d2_copy, chunk)
+            both(d1_copy, chunk)
+
+    @pl.when(even)
+    def _():
+        for chunk in range(KC):
+            both(d2_copy, chunk)
 
     for r in near:
         s2_early(r)
@@ -251,23 +261,28 @@
 
     lax.fori_loop(0, tiles, bx_start, 0)
 
+    for chunk in range(KC):
+
+        @pl.when(even)
+        def _(chunk=chunk):
+            f1_relay(chunk)
+            both(d1_copy, chunk)
+
+        for r in near:
+            s2_start(r, chunk)
+
     @pl.when(even)
     def _():
-        f1_relay(0)
-
-    for r in near:
-        s2_start(r, 0)
-
-    @pl.when(even)
-    def _():
-        f1_relay(1)
-        s1_start()
+        f1_relay(KC)
+        both(d2_copy, KC)
+        both(d1_copy, KC)
 
     for t in range(2):
         bx_copy(tile_a(t)).wait_recv()
         bt_start(tile_a(t), t)
     for r in near:
-        s2_wait(ym(r), 0)
+        for chunk in range(KC):
+            s2_wait(ym(r), chunk)
         s3_start(ym(r), 0)
 
     def dest(d):
@@ -320,40 +335,41 @@
         def _():
             bx_copy(tile_a(t + 2)).wait_recv()
 
-        @pl.when(t == NT)
+        @pl.when(t == 4)
         def _():
             for r in near:
-                s2_start(r, 1)
+                s2_start(r, KC)
 
     a_pass(0, tile_a, first_pass)
+
+    @pl.when(odd)
+    def _():
+        for chunk in range(KC + 1):
+            f1_relay(chunk)
+
     for r in near:
-        s2_wait(ym(r), 1)
+        s2_wait(ym(r), KC)
         s3_start(ym(r), 1)
     a_pass(1, tile_a)
-
-    @pl.when(odd)
-    def _():
-        f1_relay(0)
-        f1_relay(1)
-
+    for chunk in range(KC + 1):
+        s1_wait(2, chunk)
+    s2b_start()
     for r in near:
         s3_wait(ym(r), 0)
     a_pass(2, tile_a)
-    for piece in range(2):
-        s1_wait(2, piece)
-    s2b_start()
+    f2_relay()
     for r in near:
         s3_wait(ym(r), 1)
         s4_start(ym(r))
     a_pass(3, tile_a)
-    f2_relay()
     for r in near:
         s4_wait(ym(r))
     a_pass(4, tile_b)
     f2_wait()
     for piece in range(2):
         s3_start(ym(2), piece)
-        s1_wait(0, piece)
+    for chunk in range(KC + 1):
+        s1_wait(0, chunk)
     from_a(y, 0, q, lambda src: own_copy(src).start())
 
     def b_pass(i, nxt):
@@ -413,46 +429,50 @@
             ra_start(1 - d, (t + 1) // 2, 1 - d)
 
         ra_copy(d, k, d).wait()
-        rat[d] = jnp.dot(af[y], bt[slot], preferred_element_type=F32) + rat[d]
-        c_copy(d, k).wait_recv()
+        for i in range(len(B_ROWS)):
+            b_copy(d, k, i).wait_send()
+        sb[d, k] = jnp.dot(af[y], bt[slot], preferred_element_type=F32) + rat[d]
+
+    run(tile_b, None, own_work)
+
+    def last_work(t, _):
+        d, k = lax.rem(t, 2), t // 2
 
         @pl.when(t >= 2)
         def _():
             for cp in ct_copies(d, k, d):
                 cp.wait()
 
-        ct[d] = (rat[d] + rc[d, k]).astype(ct.dtype)
+        c_copy(d, k).wait_recv()
+        ct[d] = (sb[d, k] + rc[d, k]).astype(ct.dtype)
         for cp in ct_copies(d, k, d):
             cp.start()
-
-    run(tile_b, None, own_work)
+        return 0
+
+    lax.fori_loop(0, tiles, last_work, 0)
     for d in range(2):
         for cp in ct_copies(d, NT - 1, d):
             cp.wait()
 
     for side in range(2):
-        for piece in range(2):
+        for chunk in range(KC + 1):
             for make in (d1_copy, d2_copy, f1_copy):
-                make(side, piece).wait_send()
+                make(side, chunk).wait_send()
         rcopy(f2.at[side], f2.at[side], s2b_send.at[side], f2_recv.at[side], ri=y).wait_send()
         f2_copy(side).wait_send()
-    for piece in range(2):
+    for chunk in range(KC + 1):
         for r in near:
-            first, n = SUB[piece]
-            s2_copy(r, piece, s1.at[y, pl.ds(first, n)]).wait_send()
+            s2_copy(r, chunk, s1_part(y, chunk)).wait_send()
     for m in range(ny):
         for side in range(2):
             for piece in range(2):
                 s3_copy(m, side, piece).wait_send()
-        for i in range(3):
+        for i in range(2):
             s4_copy(m, i).wait_send()
 
     def drain(t, _):
-        d, k = lax.rem(t, 2), t // 2
         bx_copy(t).wait_send()
-        for i in range(len(B_ROWS)):
-            b_copy(d, k, i).wait_send()
-        c_copy(d, k).wait_send()
+        c_copy(lax.rem(t, 2), t // 2).wait_send()
         return 0
 
     lax.fori_loop(0, tiles, drain, 0)
@@ -491,8 +511,9 @@
                 pltpu.VMEM((2, rows, w), F32),
                 pltpu.VMEM((2, rows, w), jnp.bfloat16),
                 dma((2 * NT,)), dma((2 * NT,)), dma((3, 2)),
-                dma((2, 2)), dma((nx, 2, 2)), dma((2, 2)), dma((2, 2)), dma((2, 2)), dma((ny, 2)), dma((ny, 2)), dma,
-                dma((2,)), dma((2,)), dma((2,)), dma((ny, 2, 2)), dma((ny, 2, 2)), dma((ny, 3)), dma((ny, 3)),
+                dma((2, KC + 1)), dma((nx, KC + 1, 2)), dma((2, KC + 1)), dma((2, KC + 1)), dma((2, KC + 1)),
+                dma((ny, KC + 1)), dma((ny, KC + 1)), dma,
+                dma((2,)), dma((2,)), dma((2,)), dma((ny, 2, 2)), dma((ny, 2, 2)), dma((ny, 2)), dma((ny, 2)),
                 dma((2, NT, 5)), dma((2, NT, 5)), dma((2, NT, 2)), dma((2, NT, 2)), dma((2, NT)), dma((2, NT)),
                 dma((2,)), dma((2, 6)),
             ],

time: 374 us -> 371 us (level)
  no operation moved by 1% of the time
where the time goes in v3:
time: 371 us; the launch traced here: 370 us
  Pallas kernels  365 us (98%)
  local copies, waits for them, and re-layouts  5.05 us (1%)
    pallas_call x1, Pallas kernels, local_block(): pl.pallas_call(functools.partial(kernel, ny, nx), out_shape=[jax.ShapeDty...  365 us

profile of v3, /device:TPU:97, one launch (start us, length us, event | category | flops | bytes accessed | tf_op | source)
XLA Modules:
  0.0 370.4 jit_solution(1760899145820506674)
XLA Ops:
  0.0 365.3 %shard_map.28 = (bf16[384,6144]{1,0:T(8,128)(2,1)}, bf16[2048,6144]{1,0:T(8,128)(2,1)}, bf16[4,96,4096]{2,1,0:T(8,128)(2,1)}, bf16[2,48,4096]{2,1,0:T(8,128)(2,1...) custom-call(bf16[384,4096]{1,0:T(8,128)(2,1)} %a_ref.1, bf16[2048,6144]{1,0:T(8,128)(2,1)} %b_ref.1), custom_call_target="tpu_custom_call" | custom-call | tf_op jit(solution)/shard_map/pallas_call | solution.py:492
  365.3 5.1 %copy.4 = bf16[384,6144]{1,0:T(8,128)(2,1)} copy(bf16[384,6144]{1,0:T(8,128)(2,1)} %get-tuple-element.6) | data formatting | bytes 9437184
